TPU v7x, 128 devices: a whole 4x4x4 slice. The times are simulated.
128 devices in a mesh: gx: 32 (over x, y, core), gy: 4 (over z).
Axes of the slice: x: 4, y: 4, z: 4, core: 2. Of those that a mesh axis runs over, the one named last changes fastest.
Arguments:
- signals: float32 [64, 32, 16, 128], P('gx', 'gy'), may hold values from -6 to 6
- tiles: bfloat16 [64, 32, 4, 128, 128], P('gx', 'gy'), may hold values from 0 to 0.00390625
- tile_dir: int32 [64, 32, 4], P('gx', 'gy'), may hold values from 0 to 8
- tile_mask: int32 [64, 32, 4], P('gx', 'gy'), may hold values 0 or 1
- live_rows: int32 [64, 32], P('gx', 'gy'), may hold values from 32 to 128
- bound_rows: int32 [64, 32], P('gx', 'gy'), may hold values from 1 to 32, as said below
- scale_coeffs: float32 [6, 5], replicated, may hold values from -1 to 1
- spectral_bound: float32 [1], replicated, may hold values from 2.5 to 4
Outputs:
- coefficients: float32 [6, 64, 32, 16, 128], P(None, 'gx', 'gy')
- energy: float32 [6, 16], replicated
Inputs may be any that keep to these rules, and one draw needn't show every extreme that they name: `bound_rows`: in every draw, some blocks on every device have exactly 32 boundary rows.
All inputs are finite; a program needn't handle non-finite values. No bound on the sum of `tile_mask` on one device may be relied on, other than what follows from the above.
Results may differ from a plain program's by a relative error of at most 0.0003.
Values may be sent and summed in bfloat16 or wider, within the bound.
No kernel may reach another device: no remote copies, remote signals or barrier semaphores. Data moves between devices by JAX's collectives and lax.ppermute only.
A program may use at most 64 MiB of HBM per device.

v0:
```python
import jax
import jax.numpy as jnp
from jax import lax
from jax.sharding import Mesh
from jax.sharding import PartitionSpec as P

DEG = 4
GX_GY = ("gx_0", "gx_1", "gx_2", "gy")
GX = ("gx_0", "gx_1", "gx_2")


def with_halo(array, sides, width):
    for axis, dim in sides:
        devices, length = (lax.axis_size(axis), array.shape[dim])
        up = [(i, (i + 1) % devices) for i in range(devices - 1)]
        down = [(j, i) for i, j in up]
        last = lax.slice_in_dim(array, length - width, length, axis=dim)
        first = lax.slice_in_dim(array, 0, width, axis=dim)
        before = lax.ppermute(last, axis, up)
        after = lax.ppermute(first, axis, down)
        array = jnp.concatenate([before, array, after], axis=dim)
    return array


def over_axes(array, axes):
    for axis in axes:
        array = lax.psum(array, axis)
    return array


def scaled_laplacian(values, adjacent, degree, factor):
    return factor * (degree * values - adjacent) - values


def shards(
    signals, tiles, tile_dir, tile_mask, live_rows, bound_rows, scale_coeffs, spectral_bound
):
    tile_size = signals.shape[3]
    extent_x = signals.shape[0]
    extent_y = signals.shape[1]
    slot_count = tiles.shape[2]
    block_count = extent_x * extent_y
    positions = lax.broadcasted_iota(jnp.int32, (1, 1, tile_size), 2)
    live_ind = (positions < live_rows[:, :, None]).astype(jnp.float32)
    bound_ind = (positions < bound_rows[:, :, None]).astype(jnp.float32)
    flat_tiles = tiles.reshape(block_count, slot_count, tile_size, tile_size)

    def adjacency(values):
        own_rows = values.astype(jnp.bfloat16)
        edge_rows = (values * bound_ind[:, :, None, :]).astype(jnp.bfloat16)
        padded = with_halo(edge_rows, ((GX, 0), ("gy", 1)), 1)
        slot_list = []
        for slot_index in range(slot_count):
            picked = jnp.zeros_like(own_rows)
            for direction in range(9):
                step_x = direction // 3 - 1
                step_y = direction % 3 - 1
                if direction == 4:
                    source = own_rows
                else:
                    source = padded[
                        1 + step_x : 1 + step_x + extent_x, 1 + step_y : 1 + step_y + extent_y
                    ]
                matches = (tile_dir[:, :, slot_index] == direction)[:, :, None, None]
                picked = jnp.where(matches, source, picked)
            kept = (tile_mask[:, :, slot_index] == 1)[:, :, None, None]
            picked = jnp.where(kept, picked, jnp.zeros_like(picked))
            slot_list.append(picked)
        inputs = jnp.stack(slot_list, axis=1 + 1)
        flat_inputs = inputs.reshape(block_count, slot_count, inputs.shape[3], tile_size)
        product = lax.dot_general(
            flat_inputs,
            flat_tiles,
            (((1, 3), (1, 3)), ((0,), (0,))),
            preferred_element_type=jnp.float32,
        )
        product = product.reshape(extent_x, extent_y, inputs.shape[3], tile_size)
        return product * live_ind[:, :, None, :]

    channels = signals.shape[2]
    initial = signals * live_ind[:, :, None, :]
    joined = jnp.concatenate([initial, live_ind[:, :, None, :]], axis=2)
    first_pass = adjacency(joined)
    degree = first_pass[:, :, channels:, :]
    factor = 2.0 / spectral_bound[0]
    previous = initial
    current = scaled_laplacian(initial, first_pass[:, :, :channels, :], degree, factor)
    totals = 0.5 * scale_coeffs[:, 0][:, None, None, None, None] * initial[None]
    totals = totals + scale_coeffs[:, 1][:, None, None, None, None] * current[None]
    for degree_index in range(2, DEG + 1):
        adjacent = adjacency(current)
        following = 2.0 * scaled_laplacian(current, adjacent, degree, factor) - previous
        previous = current
        current = following
        totals = totals + scale_coeffs[:, degree_index][:, None, None, None, None] * current[None]
    nodes = extent_x * extent_y * tile_size * lax.axis_size(GX) * lax.axis_size("gy")
    local_sums = jnp.sum(totals * totals, axis=(1, 2, 4))
    energy = over_axes(local_sums, GX_GY) / nodes
    return (totals, energy)


def solution(mesh):
    torus = Mesh(mesh.devices.reshape(4, 4, 2, mesh.shape["gy"]), ("gx_0", "gx_1", "gx_2", "gy"))
    placed = (
        P(GX, "gy", None, None),
        P(GX, "gy", None, None, None),
        P(GX, "gy", None),
        P(GX, "gy", None),
        P(GX, "gy"),
        P(GX, "gy"),
        P(),
        P(),
    )
    return jax.shard_map(
        shards,
        mesh=torus,
        in_specs=placed,
        out_specs=(P(None, GX, "gy", None, None), P()),
        check_vma=False,
    )
```

profile of v0, /device:TPU:8, one launch (start us, length us, event | category | flops | bytes accessed | tf_op | source)
XLA Modules:
  0.0 114.4 jit_solution(3090985521356103053)
XLA Ops:
  0.6 0.9 compare_convert_fusion
  1.6 0.8 fusion.35
  2.3 0.9 broadcast_multiply_fusion.1
  3.3 1.9 %collective-permute-start = (bf16[1,8,17,128]{3,2,1,0:T(8,128)(2,1)S(1)}, bf16[1,8,17,128]{3,2,1,0:T(8,128)(2,1)S(1)}, u32[]{:S(2)}, u32[]{:S(2)}) collective-permute-start(bf16[1,8,17,128]{3,2,1,0:T(8,128)(2,1)S(1)} %get-tuple-element.37), channel_id=1, source_target_pairs={{0,4},{4,8},{8,12},{12,16},{16,20},{20,24},{24,28},{28,32},{32,36}... | collective-permute-start | bytes 104456 | tf_op jit(solution)/shard_map/ppermute | solution.py:19
  5.2 3.6 %collective-permute-start.1 = (bf16[1,8,17,128]{3,2,1,0:T(8,128)(2,1)S(1)}, bf16[1,8,17,128]{3,2,1,0:T(8,128)(2,1)S(1)}, u32[]{:S(2)}, u32[]{:S(2)}) collective-permute-start(bf16[1,8,17,128]{3,2,1,0:T(8,128)(2,1)S(1)} %get-tuple-element.38), channel_id=1, source_target_pairs={{4,0},{8,4},{12,8},{16,12},{20,16},{24,20},{28,24},{32,28},{36,32}... | collective-permute-start | bytes 104456 | tf_op jit(solution)/shard_map/ppermute | solution.py:20
  8.9 0.8 broadcast_compare_fusion.30
  9.7 0.8 broadcast_compare_fusion.31
  10.5 0.8 slice_compare_fusion.3
  11.7 1.3 %collective-permute-start.2 = (bf16[4,1,17,128]{3,2,1,0:T(8,128)(2,1)S(1)}, bf16[4,1,17,128]{3,2,1,0:T(8,128)(2,1)S(1)}, u32[]{:S(2)}, u32[]{:S(2)}) collective-permute-start(bf16[4,1,17,128]{3,2,1,0:T(8,128)(2,1)S(1)} %get-tuple-element.23), channel_id=1, source_target_pairs={{1,0},{2,1},{3,2},{5,4},{6,5},{7,6},{9,8},{10,9},{11,10},{13,12},{... | collective-permute-start | bytes 52232 | tf_op jit(solution)/shard_map/ppermute | solution.py:20
  13.0 4.5 %collective-permute-start.3 = (bf16[4,1,17,128]{3,2,1,0:T(8,128)(2,1)S(1)}, bf16[4,1,17,128]{3,2,1,0:T(8,128)(2,1)S(1)}, u32[]{:S(2)}, u32[]{:S(2)}) collective-permute-start(bf16[4,1,17,128]{3,2,1,0:T(8,128)(2,1)S(1)} %get-tuple-element.24), channel_id=1, source_target_pairs={{0,1},{1,2},{2,3},{4,5},{5,6},{6,7},{8,9},{9,10},{10,11},{12,13},{... | collective-permute-start | bytes 52232 | tf_op jit(solution)/shard_map/ppermute | solution.py:19
  18.3 0.8 collective-permute-done.3
  19.1 0.2 select_select_fusion
  19.4 0.2 select_select_fusion.3
  19.7 0.2 select_select_fusion.2
  19.9 0.2 select_select_fusion.1
  20.2 0.7 fusion
  21.0 1.9 %collective-permute-start.4 = (bf16[1,8,16,128]{3,2,1,0:T(8,128)(2,1)S(1)}, bf16[1,8,16,128]{3,2,1,0:T(8,128)(2,1)S(1)}, u32[]{:S(2)}, u32[]{:S(2)}) collective-permute-start(bf16[1,8,16,128]{3,2,1,0:T(8,128)(2,1)S(1)} %get-tuple-element.43), channel_id=1, source_target_pairs={{0,4},{4,8},{8,12},{12,16},{16,20},{20,24},{24,28},{28,32},{32,36}... | collective-permute-start | bytes 98312 | tf_op jit(solution)/shard_map/ppermute | solution.py:19
  22.9 3.6 %collective-permute-start.5 = (bf16[1,8,16,128]{3,2,1,0:T(8,128)(2,1)S(1)}, bf16[1,8,16,128]{3,2,1,0:T(8,128)(2,1)S(1)}, u32[]{:S(2)}, u32[]{:S(2)}) collective-permute-start(bf16[1,8,16,128]{3,2,1,0:T(8,128)(2,1)S(1)} %get-tuple-element.44), channel_id=1, source_target_pairs={{4,0},{8,4},{12,8},{16,12},{20,16},{24,20},{28,24},{32,28},{36,32}... | collective-permute-start | bytes 98312 | tf_op jit(solution)/shard_map/ppermute | solution.py:20
  26.6 1.6 %collective-permute-done.5 = bf16[1,8,16,128]{3,2,1,0:T(8,128)(2,1)S(1)} collective-permute-done((bf16[1,8,16,128]{3,2,1,0:T(8,128)(2,1)S(1)}, bf16[1,8,16,128]{3,2,1,0:T(8,128)(2,1)S(1)}, u32[]{:S(2)}, u32[]{:S(2)}) %collective-permute-start.5) | collective-permute-done | bytes 32800 | tf_op jit(solution)/shard_map/ppermute | solution.py:20
  28.1 1.3 %collective-permute-start.6 = (bf16[4,1,16,128]{3,2,1,0:T(8,128)(2,1)S(1)}, bf16[4,1,16,128]{3,2,1,0:T(8,128)(2,1)S(1)}, u32[]{:S(2)}, u32[]{:S(2)}) collective-permute-start(bf16[4,1,16,128]{3,2,1,0:T(8,128)(2,1)S(1)} %get-tuple-element.35), channel_id=1, source_target_pairs={{1,0},{2,1},{3,2},{5,4},{6,5},{7,6},{9,8},{10,9},{11,10},{13,12},{... | collective-permute-start | bytes 49160 | tf_op jit(solution)/shard_map/ppermute | solution.py:20
  29.4 4.8 %collective-permute-start.7 = (bf16[4,1,16,128]{3,2,1,0:T(8,128)(2,1)S(1)}, bf16[4,1,16,128]{3,2,1,0:T(8,128)(2,1)S(1)}, u32[]{:S(2)}, u32[]{:S(2)}) collective-permute-start(bf16[4,1,16,128]{3,2,1,0:T(8,128)(2,1)S(1)} %get-tuple-element.36), channel_id=1, source_target_pairs={{0,1},{1,2},{2,3},{4,5},{5,6},{6,7},{8,9},{9,10},{10,11},{12,13},{... | collective-permute-start | bytes 49160 | tf_op jit(solution)/shard_map/ppermute | solution.py:19
  34.3 1.4 %collective-permute-done.7 = bf16[4,1,16,128]{3,2,1,0:T(8,128)(2,1)S(1)} collective-permute-done((bf16[4,1,16,128]{3,2,1,0:T(8,128)(2,1)S(1)}, bf16[4,1,16,128]{3,2,1,0:T(8,128)(2,1)S(1)}, u32[]{:S(2)}, u32[]{:S(2)}) %collective-permute-start.7) | collective-permute-done | bytes 16416 | tf_op jit(solution)/shard_map/ppermute | solution.py:19
  35.7 0.2 select_select_fusion.15
  36.0 0.2 select_select_fusion.13
  36.5 0.2 select_select_fusion.12
  36.7 0.6 fusion.8
  37.5 2.7 %collective-permute-start.8 = (bf16[1,8,16,128]{3,2,1,0:T(8,128)(2,1)S(1)}, bf16[1,8,16,128]{3,2,1,0:T(8,128)(2,1)S(1)}, u32[]{:S(2)}, u32[]{:S(2)}) collective-permute-start(bf16[1,8,16,128]{3,2,1,0:T(8,128)(2,1)S(1)} %get-tuple-element.41), channel_id=1, source_target_pairs={{0,4},{4,8},{8,12},{12,16},{16,20},{20,24},{24,28},{28,32},{32,36}... | collective-permute-start | bytes 98312 | tf_op jit(solution)/shard_map/ppermute | solution.py:19
  40.2 2.8 %collective-permute-start.9 = (bf16[1,8,16,128]{3,2,1,0:T(8,128)(2,1)S(1)}, bf16[1,8,16,128]{3,2,1,0:T(8,128)(2,1)S(1)}, u32[]{:S(2)}, u32[]{:S(2)}) collective-permute-start(bf16[1,8,16,128]{3,2,1,0:T(8,128)(2,1)S(1)} %get-tuple-element.42), channel_id=1, source_target_pairs={{4,0},{8,4},{12,8},{16,12},{20,16},{24,20},{28,24},{32,28},{36,32}... | collective-permute-start | bytes 98312 | tf_op jit(solution)/shard_map/ppermute | solution.py:20
  43.1 1.6 %collective-permute-done.9 = bf16[1,8,16,128]{3,2,1,0:T(8,128)(2,1)S(1)} collective-permute-done((bf16[1,8,16,128]{3,2,1,0:T(8,128)(2,1)S(1)}, bf16[1,8,16,128]{3,2,1,0:T(8,128)(2,1)S(1)}, u32[]{:S(2)}, u32[]{:S(2)}) %collective-permute-start.9) | collective-permute-done | bytes 32800 | tf_op jit(solution)/shard_map/ppermute | solution.py:20
  44.6 1.3 %collective-permute-start.10 = (bf16[4,1,16,128]{3,2,1,0:T(8,128)(2,1)S(1)}, bf16[4,1,16,128]{3,2,1,0:T(8,128)(2,1)S(1)}, u32[]{:S(2)}, u32[]{:S(2)}) collective-permute-start(bf16[4,1,16,128]{3,2,1,0:T(8,128)(2,1)S(1)} %get-tuple-element.31), channel_id=1, source_target_pairs={{1,0},{2,1},{3,2},{5,4},{6,5},{7,6},{9,8},{10,9},{11,10},{13,12},{... | collective-permute-start | bytes 49160 | tf_op jit(solution)/shard_map/ppermute | solution.py:20
  45.9 4.8 %collective-permute-start.11 = (bf16[4,1,16,128]{3,2,1,0:T(8,128)(2,1)S(1)}, bf16[4,1,16,128]{3,2,1,0:T(8,128)(2,1)S(1)}, u32[]{:S(2)}, u32[]{:S(2)}) collective-permute-start(bf16[4,1,16,128]{3,2,1,0:T(8,128)(2,1)S(1)} %get-tuple-element.32), channel_id=1, source_target_pairs={{0,1},{1,2},{2,3},{4,5},{5,6},{6,7},{8,9},{9,10},{10,11},{12,13},{... | collective-permute-start | bytes 49160 | tf_op jit(solution)/shard_map/ppermute | solution.py:19
  50.8 1.4 %collective-permute-done.11 = bf16[4,1,16,128]{3,2,1,0:T(8,128)(2,1)S(1)} collective-permute-done((bf16[4,1,16,128]{3,2,1,0:T(8,128)(2,1)S(1)}, bf16[4,1,16,128]{3,2,1,0:T(8,128)(2,1)S(1)}, u32[]{:S(2)}, u32[]{:S(2)}) %collective-permute-start.11) | collective-permute-done | bytes 16416 | tf_op jit(solution)/shard_map/ppermute | solution.py:19
  52.2 0.2 select_select_fusion.11
  53.2 0.6 fusion.16
  54.0 2.7 %collective-permute-start.12 = (bf16[1,8,16,128]{3,2,1,0:T(8,128)(2,1)S(1)}, bf16[1,8,16,128]{3,2,1,0:T(8,128)(2,1)S(1)}, u32[]{:S(2)}, u32[]{:S(2)}) collective-permute-start(bf16[1,8,16,128]{3,2,1,0:T(8,128)(2,1)S(1)} %get-tuple-element.39), channel_id=1, source_target_pairs={{0,4},{4,8},{8,12},{12,16},{16,20},{20,24},{24,28},{28,32},{32,36}... | collective-permute-start | bytes 98312 | tf_op jit(solution)/shard_map/ppermute | solution.py:19
  56.7 2.8 %collective-permute-start.13 = (bf16[1,8,16,128]{3,2,1,0:T(8,128)(2,1)S(1)}, bf16[1,8,16,128]{3,2,1,0:T(8,128)(2,1)S(1)}, u32[]{:S(2)}, u32[]{:S(2)}) collective-permute-start(bf16[1,8,16,128]{3,2,1,0:T(8,128)(2,1)S(1)} %get-tuple-element.40), channel_id=1, source_target_pairs={{4,0},{8,4},{12,8},{16,12},{20,16},{24,20},{28,24},{32,28},{36,32}... | collective-permute-start | bytes 98312 | tf_op jit(solution)/shard_map/ppermute | solution.py:20
  59.6 1.6 %collective-permute-done.13 = bf16[1,8,16,128]{3,2,1,0:T(8,128)(2,1)S(1)} collective-permute-done((bf16[1,8,16,128]{3,2,1,0:T(8,128)(2,1)S(1)}, bf16[1,8,16,128]{3,2,1,0:T(8,128)(2,1)S(1)}, u32[]{:S(2)}, u32[]{:S(2)}) %collective-permute-start.13) | collective-permute-done | bytes 32800 | tf_op jit(solution)/shard_map/ppermute | solution.py:20
  61.1 1.3 %collective-permute-start.14 = (bf16[4,1,16,128]{3,2,1,0:T(8,128)(2,1)S(1)}, bf16[4,1,16,128]{3,2,1,0:T(8,128)(2,1)S(1)}, u32[]{:S(2)}, u32[]{:S(2)}) collective-permute-start(bf16[4,1,16,128]{3,2,1,0:T(8,128)(2,1)S(1)} %get-tuple-element.27), channel_id=1, source_target_pairs={{1,0},{2,1},{3,2},{5,4},{6,5},{7,6},{9,8},{10,9},{11,10},{13,12},{... | collective-permute-start | bytes 49160 | tf_op jit(solution)/shard_map/ppermute | solution.py:20
  62.4 4.8 %collective-permute-start.15 = (bf16[4,1,16,128]{3,2,1,0:T(8,128)(2,1)S(1)}, bf16[4,1,16,128]{3,2,1,0:T(8,128)(2,1)S(1)}, u32[]{:S(2)}, u32[]{:S(2)}) collective-permute-start(bf16[4,1,16,128]{3,2,1,0:T(8,128)(2,1)S(1)} %get-tuple-element.28), channel_id=1, source_target_pairs={{0,1},{1,2},{2,3},{4,5},{5,6},{6,7},{8,9},{9,10},{10,11},{12,13},{... | collective-permute-start | bytes 49160 | tf_op jit(solution)/shard_map/ppermute | solution.py:19
  67.5 1.2 %collective-permute-done.15 = bf16[4,1,16,128]{3,2,1,0:T(8,128)(2,1)S(1)} collective-permute-done((bf16[4,1,16,128]{3,2,1,0:T(8,128)(2,1)S(1)}, bf16[4,1,16,128]{3,2,1,0:T(8,128)(2,1)S(1)}, u32[]{:S(2)}, u32[]{:S(2)}) %collective-permute-start.15) | collective-permute-done | bytes 16416 | tf_op jit(solution)/shard_map/ppermute | solution.py:19
  68.7 0.2 select_select_fusion.7
  69.7 0.6 fusion.24
  70.4 1.3 %multiply_reduce_fusion = (f32[6,16]{1,0:T(8,128)S(1)}, f32[6,2,8,16,128]{4,3,2,1,0:T(8,128)}) fusion(f32[2,8,16,128]{3,2,1,0:T(8,128)S(1)} %multiply_subtract_fusion, f32[6]{0:T(128)S(1)} %get-tuple-element.5, f32[2,8,16,128]{3,2,1,0:T(8,128)S(1)} %get-tuple-element.12, f32[6]{0:T(128)S(1)} %get-tuple-element.6, f32[2,8,16,128]{3,2,1,0:T(8,128)S(1)} %get-tuple-element.16, ...), kind=kLoop, calls=%fused_computation | loop fusion | flops 2162592 | bytes 1442296 | tf_op jit(solution)/shard_map/reduce_sum | solution.py:97
  71.7 10.5 %psum.28 = f32[6,16]{1,0:T(8,128)S(1)} all-reduce(f32[6,16]{1,0:T(8,128)S(1)} %get-tuple-element.7), channel_id=1, replica_groups=mesh['gx_0'=4,'gx_1'=4,'gx_2'=2,'gy'=4] {'gx_0'}, use_global_device_ids=true, to_apply=%region_1.2 | all-reduce | flops 96 | bytes 768 | tf_op jit(solution)/shard_map/psum | solution.py:27
  82.2 16.6 %psum.29 = f32[6,16]{1,0:T(8,128)S(1)} all-reduce(f32[6,16]{1,0:T(8,128)S(1)} %psum.28), channel_id=1, replica_groups=mesh['gx_0'=4,'gx_1'=4,'gx_2'=2,'gy'=4] {'gx_1'}, use_global_device_ids=true, to_apply=%region_2.3 | all-reduce | flops 96 | bytes 768 | tf_op jit(solution)/shard_map/psum | solution.py:27
  98.8 2.5 %psum.30 = f32[6,16]{1,0:T(8,128)S(1)} all-reduce(f32[6,16]{1,0:T(8,128)S(1)} %psum.29), channel_id=1, replica_groups=mesh['gx_0'=4,'gx_1'=4,'gx_2'=2,'gy'=4] {'gx_2'}, use_global_device_ids=true, to_apply=%region_3.4 | all-reduce | flops 96 | bytes 768 | tf_op jit(solution)/shard_map/psum | solution.py:27
  101.2 12.6 %psum.31 = f32[6,16]{1,0:T(8,128)S(1)} all-reduce(f32[6,16]{1,0:T(8,128)S(1)} %psum.30), channel_id=1, replica_groups=mesh['gx_0'=4,'gx_1'=4,'gx_2'=2,'gy'=4] {'gy'}, use_global_device_ids=true, to_apply=%region_4.5 | all-reduce | flops 96 | bytes 768 | tf_op jit(solution)/shard_map/psum | solution.py:27
  113.8 0.6 broadcast_multiply_fusion.2
  (63 shorter events, 2.6 us)
Async XLA Ops:
  0.6 19.6 %copy-start = (bf16[2,8,4,128,128]{4,3,2,1,0:T(8,128)(2,1)S(1)}, bf16[2,8,4,128,128]{4,3,2,1,0:T(8,128)(2,1)}, u32[]{:S(2)}) copy-start(bf16[2,8,4,128,128]{4,3,2,1,0:T(8,128)(2,1)} %param.9) | copy-start | bytes 6291460
  3.3 8.4 %collective-permute-start = (bf16[1,8,17,128]{3,2,1,0:T(8,128)(2,1)S(1)}, bf16[1,8,17,128]{3,2,1,0:T(8,128)(2,1)S(1)}, u32[]{:S(2)}, u32[]{:S(2)}) collective-permute-start(bf16[1,8,17,128]{3,2,1,0:T(8,128)(2,1)S(1)} %get-tuple-element.37), channel_id=1, source_target_pairs={{0,4},{4,8},{8,12},{12,16},{16,20},{20,24},{24,28},{28,32},{32,36}... | collective-permute-start | bytes 104456 | tf_op jit(solution)/shard_map/ppermute | solution.py:19
  5.2 6.4 %collective-permute-start.1 = (bf16[1,8,17,128]{3,2,1,0:T(8,128)(2,1)S(1)}, bf16[1,8,17,128]{3,2,1,0:T(8,128)(2,1)S(1)}, u32[]{:S(2)}, u32[]{:S(2)}) collective-permute-start(bf16[1,8,17,128]{3,2,1,0:T(8,128)(2,1)S(1)} %get-tuple-element.38), channel_id=1, source_target_pairs={{4,0},{8,4},{12,8},{16,12},{20,16},{24,20},{28,24},{32,28},{36,32}... | collective-permute-start | bytes 104456 | tf_op jit(solution)/shard_map/ppermute | solution.py:20
  11.7 6.6 %collective-permute-start.2 = (bf16[4,1,17,128]{3,2,1,0:T(8,128)(2,1)S(1)}, bf16[4,1,17,128]{3,2,1,0:T(8,128)(2,1)S(1)}, u32[]{:S(2)}, u32[]{:S(2)}) collective-permute-start(bf16[4,1,17,128]{3,2,1,0:T(8,128)(2,1)S(1)} %get-tuple-element.23), channel_id=1, source_target_pairs={{1,0},{2,1},{3,2},{5,4},{6,5},{7,6},{9,8},{10,9},{11,10},{13,12},{... | collective-permute-start | bytes 52232 | tf_op jit(solution)/shard_map/ppermute | solution.py:20
  13.0 6.1 %collective-permute-start.3 = (bf16[4,1,17,128]{3,2,1,0:T(8,128)(2,1)S(1)}, bf16[4,1,17,128]{3,2,1,0:T(8,128)(2,1)S(1)}, u32[]{:S(2)}, u32[]{:S(2)}) collective-permute-start(bf16[4,1,17,128]{3,2,1,0:T(8,128)(2,1)S(1)} %get-tuple-element.24), channel_id=1, source_target_pairs={{0,1},{1,2},{2,3},{4,5},{5,6},{6,7},{8,9},{9,10},{10,11},{12,13},{... | collective-permute-start | bytes 52232 | tf_op jit(solution)/shard_map/ppermute | solution.py:19
  19.9 1.0 copy-start.1
  21.0 5.6 %collective-permute-start.4 = (bf16[1,8,16,128]{3,2,1,0:T(8,128)(2,1)S(1)}, bf16[1,8,16,128]{3,2,1,0:T(8,128)(2,1)S(1)}, u32[]{:S(2)}, u32[]{:S(2)}) collective-permute-start(bf16[1,8,16,128]{3,2,1,0:T(8,128)(2,1)S(1)} %get-tuple-element.43), channel_id=1, source_target_pairs={{0,4},{4,8},{8,12},{12,16},{16,20},{20,24},{24,28},{28,32},{32,36}... | collective-permute-start | bytes 98312 | tf_op jit(solution)/shard_map/ppermute | solution.py:19
  22.9 5.2 %collective-permute-start.5 = (bf16[1,8,16,128]{3,2,1,0:T(8,128)(2,1)S(1)}, bf16[1,8,16,128]{3,2,1,0:T(8,128)(2,1)S(1)}, u32[]{:S(2)}, u32[]{:S(2)}) collective-permute-start(bf16[1,8,16,128]{3,2,1,0:T(8,128)(2,1)S(1)} %get-tuple-element.44), channel_id=1, source_target_pairs={{4,0},{8,4},{12,8},{16,12},{20,16},{24,20},{28,24},{32,28},{36,32}... | collective-permute-start | bytes 98312 | tf_op jit(solution)/shard_map/ppermute | solution.py:20
  28.1 6.1 %collective-permute-start.6 = (bf16[4,1,16,128]{3,2,1,0:T(8,128)(2,1)S(1)}, bf16[4,1,16,128]{3,2,1,0:T(8,128)(2,1)S(1)}, u32[]{:S(2)}, u32[]{:S(2)}) collective-permute-start(bf16[4,1,16,128]{3,2,1,0:T(8,128)(2,1)S(1)} %get-tuple-element.35), channel_id=1, source_target_pairs={{1,0},{2,1},{3,2},{5,4},{6,5},{7,6},{9,8},{10,9},{11,10},{13,12},{... | collective-permute-start | bytes 49160 | tf_op jit(solution)/shard_map/ppermute | solution.py:20
  29.4 6.3 %collective-permute-start.7 = (bf16[4,1,16,128]{3,2,1,0:T(8,128)(2,1)S(1)}, bf16[4,1,16,128]{3,2,1,0:T(8,128)(2,1)S(1)}, u32[]{:S(2)}, u32[]{:S(2)}) collective-permute-start(bf16[4,1,16,128]{3,2,1,0:T(8,128)(2,1)S(1)} %get-tuple-element.36), channel_id=1, source_target_pairs={{0,1},{1,2},{2,3},{4,5},{5,6},{6,7},{8,9},{9,10},{10,11},{12,13},{... | collective-permute-start | bytes 49160 | tf_op jit(solution)/shard_map/ppermute | solution.py:19
  37.5 5.6 %collective-permute-start.8 = (bf16[1,8,16,128]{3,2,1,0:T(8,128)(2,1)S(1)}, bf16[1,8,16,128]{3,2,1,0:T(8,128)(2,1)S(1)}, u32[]{:S(2)}, u32[]{:S(2)}) collective-permute-start(bf16[1,8,16,128]{3,2,1,0:T(8,128)(2,1)S(1)} %get-tuple-element.41), channel_id=1, source_target_pairs={{0,4},{4,8},{8,12},{12,16},{16,20},{20,24},{24,28},{28,32},{32,36}... | collective-permute-start | bytes 98312 | tf_op jit(solution)/shard_map/ppermute | solution.py:19
  40.2 4.4 %collective-permute-start.9 = (bf16[1,8,16,128]{3,2,1,0:T(8,128)(2,1)S(1)}, bf16[1,8,16,128]{3,2,1,0:T(8,128)(2,1)S(1)}, u32[]{:S(2)}, u32[]{:S(2)}) collective-permute-start(bf16[1,8,16,128]{3,2,1,0:T(8,128)(2,1)S(1)} %get-tuple-element.42), channel_id=1, source_target_pairs={{4,0},{8,4},{12,8},{16,12},{20,16},{24,20},{28,24},{32,28},{36,32}... | collective-permute-start | bytes 98312 | tf_op jit(solution)/shard_map/ppermute | solution.py:20
  44.6 6.1 %collective-permute-start.10 = (bf16[4,1,16,128]{3,2,1,0:T(8,128)(2,1)S(1)}, bf16[4,1,16,128]{3,2,1,0:T(8,128)(2,1)S(1)}, u32[]{:S(2)}, u32[]{:S(2)}) collective-permute-start(bf16[4,1,16,128]{3,2,1,0:T(8,128)(2,1)S(1)} %get-tuple-element.31), channel_id=1, source_target_pairs={{1,0},{2,1},{3,2},{5,4},{6,5},{7,6},{9,8},{10,9},{11,10},{13,12},{... | collective-permute-start | bytes 49160 | tf_op jit(solution)/shard_map/ppermute | solution.py:20
  45.9 6.3 %collective-permute-start.11 = (bf16[4,1,16,128]{3,2,1,0:T(8,128)(2,1)S(1)}, bf16[4,1,16,128]{3,2,1,0:T(8,128)(2,1)S(1)}, u32[]{:S(2)}, u32[]{:S(2)}) collective-permute-start(bf16[4,1,16,128]{3,2,1,0:T(8,128)(2,1)S(1)} %get-tuple-element.32), channel_id=1, source_target_pairs={{0,1},{1,2},{2,3},{4,5},{5,6},{6,7},{8,9},{9,10},{10,11},{12,13},{... | collective-permute-start | bytes 49160 | tf_op jit(solution)/shard_map/ppermute | solution.py:19
  53.0 14.3 %copy-start.2 = (f32[6,5]{1,0:T(8,128)S(1)}, f32[6,5]{1,0:T(8,128)}, u32[]{:S(2)}) copy-start(f32[6,5]{1,0:T(8,128)} %param.14) | copy-start | bytes 364
  54.0 5.6 %collective-permute-start.12 = (bf16[1,8,16,128]{3,2,1,0:T(8,128)(2,1)S(1)}, bf16[1,8,16,128]{3,2,1,0:T(8,128)(2,1)S(1)}, u32[]{:S(2)}, u32[]{:S(2)}) collective-permute-start(bf16[1,8,16,128]{3,2,1,0:T(8,128)(2,1)S(1)} %get-tuple-element.39), channel_id=1, source_target_pairs={{0,4},{4,8},{8,12},{12,16},{16,20},{20,24},{24,28},{28,32},{32,36}... | collective-permute-start | bytes 98312 | tf_op jit(solution)/shard_map/ppermute | solution.py:19
  56.7 4.4 %collective-permute-start.13 = (bf16[1,8,16,128]{3,2,1,0:T(8,128)(2,1)S(1)}, bf16[1,8,16,128]{3,2,1,0:T(8,128)(2,1)S(1)}, u32[]{:S(2)}, u32[]{:S(2)}) collective-permute-start(bf16[1,8,16,128]{3,2,1,0:T(8,128)(2,1)S(1)} %get-tuple-element.40), channel_id=1, source_target_pairs={{4,0},{8,4},{12,8},{16,12},{20,16},{24,20},{28,24},{32,28},{36,32}... | collective-permute-start | bytes 98312 | tf_op jit(solution)/shard_map/ppermute | solution.py:20
  61.1 6.4 %collective-permute-start.14 = (bf16[4,1,16,128]{3,2,1,0:T(8,128)(2,1)S(1)}, bf16[4,1,16,128]{3,2,1,0:T(8,128)(2,1)S(1)}, u32[]{:S(2)}, u32[]{:S(2)}) collective-permute-start(bf16[4,1,16,128]{3,2,1,0:T(8,128)(2,1)S(1)} %get-tuple-element.27), channel_id=1, source_target_pairs={{1,0},{2,1},{3,2},{5,4},{6,5},{7,6},{9,8},{10,9},{11,10},{13,12},{... | collective-permute-start | bytes 49160 | tf_op jit(solution)/shard_map/ppermute | solution.py:20
  62.4 6.3 %collective-permute-start.15 = (bf16[4,1,16,128]{3,2,1,0:T(8,128)(2,1)S(1)}, bf16[4,1,16,128]{3,2,1,0:T(8,128)(2,1)S(1)}, u32[]{:S(2)}, u32[]{:S(2)}) collective-permute-start(bf16[4,1,16,128]{3,2,1,0:T(8,128)(2,1)S(1)} %get-tuple-element.28), channel_id=1, source_target_pairs={{0,1},{1,2},{2,3},{4,5},{5,6},{6,7},{8,9},{9,10},{10,11},{12,13},{... | collective-permute-start | bytes 49160 | tf_op jit(solution)/shard_map/ppermute | solution.py:19
where the time goes:
time: 115 us; the launch traced here: 114 us
  starting transfers between devices  46.4 us (40%)
  blocking collectives  42.1 us (37%)
  other arithmetic  11.6 us (10%)
  waiting for transfers between devices  9.5 us (8%)
  matrix products  2.6 us (2%)
  between operations  1.98 us (2%)
    psum x4, blocking collectives, over_axes(): array = lax.psum(array, axis)  42.1 us
    ppermute x8, starting transfers between devices, with_halo(): before = lax.ppermute(last, axis, up)  28.4 us
    ppermute x8, starting transfers between devices, with_halo(): after = lax.ppermute(first, axis, down)  18.1 us
    ppermute x8, waiting for transfers between devices, with_halo(): before = lax.ppermute(last, axis, up)  4.79 us
    ppermute x8, waiting for transfers between devices, with_halo(): after = lax.ppermute(first, axis, down)  4.71 us
    select_n x16, other arithmetic, adjacency(): picked = jnp.where(kept, picked, jnp.zeros_like(picked))  3.91 us
    dot_general x4, matrix products, adjacency(): lax.dot_general(flat_inputs, flat_tiles, (((1, 3), (1, 3)), ((0,), (0,)))...  2.6 us
  transfers between devices with their start and end apart: 16, of which 7 were waited for; matrix products, arithmetic and copies ran while one was open for 3% of the time, Pallas kernels for 0%

commit v1 on v0

--- a/solution.py
+++ b/solution.py
@@ -24,7 +24,11 @@
 
 def over_axes(array, axes):
     for axis in axes:
-        array = lax.psum(array, axis)
+
+        def _obtain_files(body):
+            return jnp.sum(lax.all_gather(body, axis), 0)
+
+        array = _obtain_files(array)
     return array
 
 

time: 115 us -> 121 us (1.052)
  the two profiles are of different devices: /device:TPU:8 before, /device:TPU:0 now
where the time goes in v1:
time: 121 us
  blocking collectives  49.3 us (41%)
  starting transfers between devices  41.7 us (34%)
  waiting for transfers between devices  13.4 us (11%)
  other arithmetic  11.6 us (10%)
  matrix products  2.6 us (2%)
  between operations  1.97 us (2%)
    all_gather x4, blocking collectives, _obtain_files(): return jnp.sum(lax.all_gather(body, axis), 0)  49.3 us
    ppermute x8, starting transfers between devices, with_halo(): before = lax.ppermute(last, axis, up)  31.4 us
    ppermute x8, starting transfers between devices, with_halo(): after = lax.ppermute(first, axis, down)  10.3 us
    ppermute x8, waiting for transfers between devices, with_halo(): after = lax.ppermute(first, axis, down)  8.58 us
    ppermute x8, waiting for transfers between devices, with_halo(): before = lax.ppermute(last, axis, up)  4.79 us
    select_n x16, other arithmetic, adjacency(): picked = jnp.where(kept, picked, jnp.zeros_like(picked))  3.91 us
    dot_general x4, matrix products, adjacency(): lax.dot_general(flat_inputs, flat_tiles, (((1, 3), (1, 3)), ((0,), (0,)))...  2.6 us
  transfers between devices with their start and end apart: 16, of which 8 were waited for; matrix products, arithmetic and copies ran while one was open for 2% of the time, Pallas kernels for 0%

profile of v1, /device:TPU:0, one launch (start us, length us, event | category | flops | bytes accessed | tf_op | source)
XLA Modules:
  0.0 120.8 jit_solution(11165109094340873988)
XLA Ops:
  0.6 0.9 compare_convert_fusion
  1.6 0.8 fusion.35
  2.3 0.9 broadcast_multiply_fusion.1
  3.3 1.3 %collective-permute-start = (bf16[1,8,17,128]{3,2,1,0:T(8,128)(2,1)S(1)}, bf16[1,8,17,128]{3,2,1,0:T(8,128)(2,1)S(1)}, u32[]{:S(2)}, u32[]{:S(2)}) collective-permute-start(bf16[1,8,17,128]{3,2,1,0:T(8,128)(2,1)S(1)} %get-tuple-element.37), channel_id=1, source_target_pairs={{0,4},{4,8},{8,12},{12,16},{16,20},{20,24},{24,28},{28,32},{32,36}... | collective-permute-start | bytes 104456 | tf_op jit(solution)/shard_map/ppermute | solution.py:19
  4.6 1.3 %collective-permute-start.1 = (bf16[1,8,17,128]{3,2,1,0:T(8,128)(2,1)S(1)}, bf16[1,8,17,128]{3,2,1,0:T(8,128)(2,1)S(1)}, u32[]{:S(2)}, u32[]{:S(2)}) collective-permute-start(bf16[1,8,17,128]{3,2,1,0:T(8,128)(2,1)S(1)} %get-tuple-element.38), channel_id=1, source_target_pairs={{4,0},{8,4},{12,8},{16,12},{20,16},{24,20},{28,24},{32,28},{36,32}... | collective-permute-start | bytes 104456 | tf_op jit(solution)/shard_map/ppermute | solution.py:20
  5.9 0.8 broadcast_compare_fusion.30
  6.7 0.8 broadcast_compare_fusion.31
  7.6 0.8 slice_compare_fusion.3
  8.7 1.0 collective-permute-done.1
  9.7 1.3 %collective-permute-start.2 = (bf16[4,1,17,128]{3,2,1,0:T(8,128)(2,1)S(1)}, bf16[4,1,17,128]{3,2,1,0:T(8,128)(2,1)S(1)}, u32[]{:S(2)}, u32[]{:S(2)}) collective-permute-start(bf16[4,1,17,128]{3,2,1,0:T(8,128)(2,1)S(1)} %get-tuple-element.23), channel_id=1, source_target_pairs={{1,0},{2,1},{3,2},{5,4},{6,5},{7,6},{9,8},{10,9},{11,10},{13,12},{... | collective-permute-start | bytes 52232 | tf_op jit(solution)/shard_map/ppermute | solution.py:20
  11.0 4.5 %collective-permute-start.3 = (bf16[4,1,17,128]{3,2,1,0:T(8,128)(2,1)S(1)}, bf16[4,1,17,128]{3,2,1,0:T(8,128)(2,1)S(1)}, u32[]{:S(2)}, u32[]{:S(2)}) collective-permute-start(bf16[4,1,17,128]{3,2,1,0:T(8,128)(2,1)S(1)} %get-tuple-element.24), channel_id=1, source_target_pairs={{0,1},{1,2},{2,3},{4,5},{5,6},{6,7},{8,9},{9,10},{10,11},{12,13},{... | collective-permute-start | bytes 52232 | tf_op jit(solution)/shard_map/ppermute | solution.py:19
  16.3 0.8 collective-permute-done.3
  17.1 0.2 select_select_fusion
  17.4 0.2 select_select_fusion.3
  17.6 0.2 select_select_fusion.2
  17.9 0.2 select_select_fusion.1
  18.2 0.7 fusion
  18.9 3.7 %collective-permute-start.4 = (bf16[1,8,16,128]{3,2,1,0:T(8,128)(2,1)S(1)}, bf16[1,8,16,128]{3,2,1,0:T(8,128)(2,1)S(1)}, u32[]{:S(2)}, u32[]{:S(2)}) collective-permute-start(bf16[1,8,16,128]{3,2,1,0:T(8,128)(2,1)S(1)} %get-tuple-element.43), channel_id=1, source_target_pairs={{0,4},{4,8},{8,12},{12,16},{16,20},{20,24},{24,28},{28,32},{32,36}... | collective-permute-start | bytes 98312 | tf_op jit(solution)/shard_map/ppermute | solution.py:19
  22.7 1.3 %collective-permute-start.5 = (bf16[1,8,16,128]{3,2,1,0:T(8,128)(2,1)S(1)}, bf16[1,8,16,128]{3,2,1,0:T(8,128)(2,1)S(1)}, u32[]{:S(2)}, u32[]{:S(2)}) collective-permute-start(bf16[1,8,16,128]{3,2,1,0:T(8,128)(2,1)S(1)} %get-tuple-element.44), channel_id=1, source_target_pairs={{4,0},{8,4},{12,8},{16,12},{20,16},{24,20},{28,24},{32,28},{36,32}... | collective-permute-start | bytes 98312 | tf_op jit(solution)/shard_map/ppermute | solution.py:20
  24.0 3.3 %collective-permute-done.5 = bf16[1,8,16,128]{3,2,1,0:T(8,128)(2,1)S(1)} collective-permute-done((bf16[1,8,16,128]{3,2,1,0:T(8,128)(2,1)S(1)}, bf16[1,8,16,128]{3,2,1,0:T(8,128)(2,1)S(1)}, u32[]{:S(2)}, u32[]{:S(2)}) %collective-permute-start.5) | collective-permute-done | bytes 32800 | tf_op jit(solution)/shard_map/ppermute | solution.py:20
  27.3 1.3 %collective-permute-start.6 = (bf16[4,1,16,128]{3,2,1,0:T(8,128)(2,1)S(1)}, bf16[4,1,16,128]{3,2,1,0:T(8,128)(2,1)S(1)}, u32[]{:S(2)}, u32[]{:S(2)}) collective-permute-start(bf16[4,1,16,128]{3,2,1,0:T(8,128)(2,1)S(1)} %get-tuple-element.35), channel_id=1, source_target_pairs={{1,0},{2,1},{3,2},{5,4},{6,5},{7,6},{9,8},{10,9},{11,10},{13,12},{... | collective-permute-start | bytes 49160 | tf_op jit(solution)/shard_map/ppermute | solution.py:20
  28.6 4.8 %collective-permute-start.7 = (bf16[4,1,16,128]{3,2,1,0:T(8,128)(2,1)S(1)}, bf16[4,1,16,128]{3,2,1,0:T(8,128)(2,1)S(1)}, u32[]{:S(2)}, u32[]{:S(2)}) collective-permute-start(bf16[4,1,16,128]{3,2,1,0:T(8,128)(2,1)S(1)} %get-tuple-element.36), channel_id=1, source_target_pairs={{0,1},{1,2},{2,3},{4,5},{5,6},{6,7},{8,9},{9,10},{10,11},{12,13},{... | collective-permute-start | bytes 49160 | tf_op jit(solution)/shard_map/ppermute | solution.py:19
  33.5 1.4 %collective-permute-done.7 = bf16[4,1,16,128]{3,2,1,0:T(8,128)(2,1)S(1)} collective-permute-done((bf16[4,1,16,128]{3,2,1,0:T(8,128)(2,1)S(1)}, bf16[4,1,16,128]{3,2,1,0:T(8,128)(2,1)S(1)}, u32[]{:S(2)}, u32[]{:S(2)}) %collective-permute-start.7) | collective-permute-done | bytes 16416 | tf_op jit(solution)/shard_map/ppermute | solution.py:19
  34.9 0.2 select_select_fusion.15
  35.2 0.2 select_select_fusion.13
  35.9 0.6 fusion.8
  36.7 3.7 %collective-permute-start.8 = (bf16[1,8,16,128]{3,2,1,0:T(8,128)(2,1)S(1)}, bf16[1,8,16,128]{3,2,1,0:T(8,128)(2,1)S(1)}, u32[]{:S(2)}, u32[]{:S(2)}) collective-permute-start(bf16[1,8,16,128]{3,2,1,0:T(8,128)(2,1)S(1)} %get-tuple-element.41), channel_id=1, source_target_pairs={{0,4},{4,8},{8,12},{12,16},{16,20},{20,24},{24,28},{28,32},{32,36}... | collective-permute-start | bytes 98312 | tf_op jit(solution)/shard_map/ppermute | solution.py:19
  40.3 1.3 %collective-permute-start.9 = (bf16[1,8,16,128]{3,2,1,0:T(8,128)(2,1)S(1)}, bf16[1,8,16,128]{3,2,1,0:T(8,128)(2,1)S(1)}, u32[]{:S(2)}, u32[]{:S(2)}) collective-permute-start(bf16[1,8,16,128]{3,2,1,0:T(8,128)(2,1)S(1)} %get-tuple-element.42), channel_id=1, source_target_pairs={{4,0},{8,4},{12,8},{16,12},{20,16},{24,20},{28,24},{32,28},{36,32}... | collective-permute-start | bytes 98312 | tf_op jit(solution)/shard_map/ppermute | solution.py:20
  41.7 2.2 %collective-permute-done.9 = bf16[1,8,16,128]{3,2,1,0:T(8,128)(2,1)S(1)} collective-permute-done((bf16[1,8,16,128]{3,2,1,0:T(8,128)(2,1)S(1)}, bf16[1,8,16,128]{3,2,1,0:T(8,128)(2,1)S(1)}, u32[]{:S(2)}, u32[]{:S(2)}) %collective-permute-start.9) | collective-permute-done | bytes 32800 | tf_op jit(solution)/shard_map/ppermute | solution.py:20
  43.8 1.3 %collective-permute-start.10 = (bf16[4,1,16,128]{3,2,1,0:T(8,128)(2,1)S(1)}, bf16[4,1,16,128]{3,2,1,0:T(8,128)(2,1)S(1)}, u32[]{:S(2)}, u32[]{:S(2)}) collective-permute-start(bf16[4,1,16,128]{3,2,1,0:T(8,128)(2,1)S(1)} %get-tuple-element.31), channel_id=1, source_target_pairs={{1,0},{2,1},{3,2},{5,4},{6,5},{7,6},{9,8},{10,9},{11,10},{13,12},{... | collective-permute-start | bytes 49160 | tf_op jit(solution)/shard_map/ppermute | solution.py:20
  45.1 4.8 %collective-permute-start.11 = (bf16[4,1,16,128]{3,2,1,0:T(8,128)(2,1)S(1)}, bf16[4,1,16,128]{3,2,1,0:T(8,128)(2,1)S(1)}, u32[]{:S(2)}, u32[]{:S(2)}) collective-permute-start(bf16[4,1,16,128]{3,2,1,0:T(8,128)(2,1)S(1)} %get-tuple-element.32), channel_id=1, source_target_pairs={{0,1},{1,2},{2,3},{4,5},{5,6},{6,7},{8,9},{9,10},{10,11},{12,13},{... | collective-permute-start | bytes 49160 | tf_op jit(solution)/shard_map/ppermute | solution.py:19
  49.9 1.4 %collective-permute-done.11 = bf16[4,1,16,128]{3,2,1,0:T(8,128)(2,1)S(1)} collective-permute-done((bf16[4,1,16,128]{3,2,1,0:T(8,128)(2,1)S(1)}, bf16[4,1,16,128]{3,2,1,0:T(8,128)(2,1)S(1)}, u32[]{:S(2)}, u32[]{:S(2)}) %collective-permute-start.11) | collective-permute-done | bytes 16416 | tf_op jit(solution)/shard_map/ppermute | solution.py:19
  51.4 0.2 select_select_fusion.11
  52.4 0.6 fusion.16
  53.1 3.7 %collective-permute-start.12 = (bf16[1,8,16,128]{3,2,1,0:T(8,128)(2,1)S(1)}, bf16[1,8,16,128]{3,2,1,0:T(8,128)(2,1)S(1)}, u32[]{:S(2)}, u32[]{:S(2)}) collective-permute-start(bf16[1,8,16,128]{3,2,1,0:T(8,128)(2,1)S(1)} %get-tuple-element.39), channel_id=1, source_target_pairs={{0,4},{4,8},{8,12},{12,16},{16,20},{20,24},{24,28},{28,32},{32,36}... | collective-permute-start | bytes 98312 | tf_op jit(solution)/shard_map/ppermute | solution.py:19
  56.8 1.3 %collective-permute-start.13 = (bf16[1,8,16,128]{3,2,1,0:T(8,128)(2,1)S(1)}, bf16[1,8,16,128]{3,2,1,0:T(8,128)(2,1)S(1)}, u32[]{:S(2)}, u32[]{:S(2)}) collective-permute-start(bf16[1,8,16,128]{3,2,1,0:T(8,128)(2,1)S(1)} %get-tuple-element.40), channel_id=1, source_target_pairs={{4,0},{8,4},{12,8},{16,12},{20,16},{24,20},{28,24},{32,28},{36,32}... | collective-permute-start | bytes 98312 | tf_op jit(solution)/shard_map/ppermute | solution.py:20
  58.1 2.2 %collective-permute-done.13 = bf16[1,8,16,128]{3,2,1,0:T(8,128)(2,1)S(1)} collective-permute-done((bf16[1,8,16,128]{3,2,1,0:T(8,128)(2,1)S(1)}, bf16[1,8,16,128]{3,2,1,0:T(8,128)(2,1)S(1)}, u32[]{:S(2)}, u32[]{:S(2)}) %collective-permute-start.13) | collective-permute-done | bytes 32800 | tf_op jit(solution)/shard_map/ppermute | solution.py:20
  60.3 1.3 %collective-permute-start.14 = (bf16[4,1,16,128]{3,2,1,0:T(8,128)(2,1)S(1)}, bf16[4,1,16,128]{3,2,1,0:T(8,128)(2,1)S(1)}, u32[]{:S(2)}, u32[]{:S(2)}) collective-permute-start(bf16[4,1,16,128]{3,2,1,0:T(8,128)(2,1)S(1)} %get-tuple-element.27), channel_id=1, source_target_pairs={{1,0},{2,1},{3,2},{5,4},{6,5},{7,6},{9,8},{10,9},{11,10},{13,12},{... | collective-permute-start | bytes 49160 | tf_op jit(solution)/shard_map/ppermute | solution.py:20
  61.6 4.8 %collective-permute-start.15 = (bf16[4,1,16,128]{3,2,1,0:T(8,128)(2,1)S(1)}, bf16[4,1,16,128]{3,2,1,0:T(8,128)(2,1)S(1)}, u32[]{:S(2)}, u32[]{:S(2)}) collective-permute-start(bf16[4,1,16,128]{3,2,1,0:T(8,128)(2,1)S(1)} %get-tuple-element.28), channel_id=1, source_target_pairs={{0,1},{1,2},{2,3},{4,5},{5,6},{6,7},{8,9},{9,10},{10,11},{12,13},{... | collective-permute-start | bytes 49160 | tf_op jit(solution)/shard_map/ppermute | solution.py:19
  66.7 1.2 collective-permute-done.15
  67.9 0.2 select_select_fusion.7
  68.9 0.6 fusion.24
  69.6 1.3 %multiply_reduce_fusion = (f32[6,16]{1,0:T(8,128)S(1)}, f32[6,2,8,16,128]{4,3,2,1,0:T(8,128)}) fusion(f32[2,8,16,128]{3,2,1,0:T(8,128)S(1)} %multiply_subtract_fusion, f32[6]{0:T(128)S(1)} %get-tuple-element.5, f32[2,8,16,128]{3,2,1,0:T(8,128)S(1)} %get-tuple-element.12, f32[6]{0:T(128)S(1)} %get-tuple-element.6, f32[2,8,16,128]{3,2,1,0:T(8,128)S(1)} %get-tuple-element.16, ...), kind=kLoop, calls=%fused_computation | loop fusion | flops 2162592 | bytes 1442296 | tf_op jit(solution)/shard_map/reduce_sum | solution.py:101
  70.9 21.7 %all-gather.4 = f32[4,6,16]{2,1,0:T(8,128)S(1)} all-gather(f32[1,6,16]{2,1,0:T(8,128)S(1)} %bitcast.153), channel_id=2, replica_groups=mesh['gx_0'=4,'gx_1'=4,'gx_2'=2,'gy'=4] {'gx_0'}, dimensions={0}, use_global_device_ids=true | all-gather | bytes 1920 | tf_op jit(solution)/shard_map/all_gather | solution.py:29
  92.6 12.0 %all-gather.5 = f32[4,6,16]{2,1,0:T(8,128)S(1)} all-gather(f32[1,6,16]{2,1,0:T(8,128)S(1)} %bitcast.155), channel_id=3, replica_groups=mesh['gx_0'=4,'gx_1'=4,'gx_2'=2,'gy'=4] {'gx_1'}, dimensions={0}, use_global_device_ids=true | all-gather | bytes 1920 | tf_op jit(solution)/shard_map/all_gather | solution.py:29
  104.6 1.8 %all-gather.6 = f32[2,6,16]{2,1,0:T(8,128)S(1)} all-gather(f32[1,6,16]{2,1,0:T(8,128)S(1)} %bitcast.156), channel_id=4, replica_groups=mesh['gx_0'=4,'gx_1'=4,'gx_2'=2,'gy'=4] {'gx_2'}, dimensions={0}, use_global_device_ids=true | all-gather | bytes 1152 | tf_op jit(solution)/shard_map/all_gather | solution.py:29
  106.5 13.7 %all-gather.7 = f32[4,6,16]{2,1,0:T(8,128)S(1)} all-gather(f32[1,6,16]{2,1,0:T(8,128)S(1)} %bitcast.154), channel_id=5, replica_groups=mesh['gx_0'=4,'gx_1'=4,'gx_2'=2,'gy'=4] {'gy'}, dimensions={0}, use_global_device_ids=true | all-gather | bytes 1920 | tf_op jit(solution)/shard_map/all_gather | solution.py:29
  120.2 0.6 broadcast_multiply_fusion.2
  (67 shorter events, 2.9 us)
Async XLA Ops:
  0.6 17.5 %copy-start = (bf16[2,8,4,128,128]{4,3,2,1,0:T(8,128)(2,1)S(1)}, bf16[2,8,4,128,128]{4,3,2,1,0:T(8,128)(2,1)}, u32[]{:S(2)}) copy-start(bf16[2,8,4,128,128]{4,3,2,1,0:T(8,128)(2,1)} %param.9) | copy-start | bytes 6291460
  3.3 5.4 %collective-permute-start = (bf16[1,8,17,128]{3,2,1,0:T(8,128)(2,1)S(1)}, bf16[1,8,17,128]{3,2,1,0:T(8,128)(2,1)S(1)}, u32[]{:S(2)}, u32[]{:S(2)}) collective-permute-start(bf16[1,8,17,128]{3,2,1,0:T(8,128)(2,1)S(1)} %get-tuple-element.37), channel_id=1, source_target_pairs={{0,4},{4,8},{8,12},{12,16},{16,20},{20,24},{24,28},{28,32},{32,36}... | collective-permute-start | bytes 104456 | tf_op jit(solution)/shard_map/ppermute | solution.py:19
  4.6 5.0 %collective-permute-start.1 = (bf16[1,8,17,128]{3,2,1,0:T(8,128)(2,1)S(1)}, bf16[1,8,17,128]{3,2,1,0:T(8,128)(2,1)S(1)}, u32[]{:S(2)}, u32[]{:S(2)}) collective-permute-start(bf16[1,8,17,128]{3,2,1,0:T(8,128)(2,1)S(1)} %get-tuple-element.38), channel_id=1, source_target_pairs={{4,0},{8,4},{12,8},{16,12},{20,16},{24,20},{28,24},{32,28},{36,32}... | collective-permute-start | bytes 104456 | tf_op jit(solution)/shard_map/ppermute | solution.py:20
  9.7 6.6 %collective-permute-start.2 = (bf16[4,1,17,128]{3,2,1,0:T(8,128)(2,1)S(1)}, bf16[4,1,17,128]{3,2,1,0:T(8,128)(2,1)S(1)}, u32[]{:S(2)}, u32[]{:S(2)}) collective-permute-start(bf16[4,1,17,128]{3,2,1,0:T(8,128)(2,1)S(1)} %get-tuple-element.23), channel_id=1, source_target_pairs={{1,0},{2,1},{3,2},{5,4},{6,5},{7,6},{9,8},{10,9},{11,10},{13,12},{... | collective-permute-start | bytes 52232 | tf_op jit(solution)/shard_map/ppermute | solution.py:20
  11.0 6.1 %collective-permute-start.3 = (bf16[4,1,17,128]{3,2,1,0:T(8,128)(2,1)S(1)}, bf16[4,1,17,128]{3,2,1,0:T(8,128)(2,1)S(1)}, u32[]{:S(2)}, u32[]{:S(2)}) collective-permute-start(bf16[4,1,17,128]{3,2,1,0:T(8,128)(2,1)S(1)} %get-tuple-element.24), channel_id=1, source_target_pairs={{0,1},{1,2},{2,3},{4,5},{5,6},{6,7},{8,9},{9,10},{10,11},{12,13},{... | collective-permute-start | bytes 52232 | tf_op jit(solution)/shard_map/ppermute | solution.py:19
  17.9 1.0 copy-start.1
  18.9 5.0 %collective-permute-start.4 = (bf16[1,8,16,128]{3,2,1,0:T(8,128)(2,1)S(1)}, bf16[1,8,16,128]{3,2,1,0:T(8,128)(2,1)S(1)}, u32[]{:S(2)}, u32[]{:S(2)}) collective-permute-start(bf16[1,8,16,128]{3,2,1,0:T(8,128)(2,1)S(1)} %get-tuple-element.43), channel_id=1, source_target_pairs={{0,4},{4,8},{8,12},{12,16},{16,20},{20,24},{24,28},{28,32},{32,36}... | collective-permute-start | bytes 98312 | tf_op jit(solution)/shard_map/ppermute | solution.py:19
  22.7 4.6 %collective-permute-start.5 = (bf16[1,8,16,128]{3,2,1,0:T(8,128)(2,1)S(1)}, bf16[1,8,16,128]{3,2,1,0:T(8,128)(2,1)S(1)}, u32[]{:S(2)}, u32[]{:S(2)}) collective-permute-start(bf16[1,8,16,128]{3,2,1,0:T(8,128)(2,1)S(1)} %get-tuple-element.44), channel_id=1, source_target_pairs={{4,0},{8,4},{12,8},{16,12},{20,16},{24,20},{28,24},{32,28},{36,32}... | collective-permute-start | bytes 98312 | tf_op jit(solution)/shard_map/ppermute | solution.py:20
  27.3 6.1 %collective-permute-start.6 = (bf16[4,1,16,128]{3,2,1,0:T(8,128)(2,1)S(1)}, bf16[4,1,16,128]{3,2,1,0:T(8,128)(2,1)S(1)}, u32[]{:S(2)}, u32[]{:S(2)}) collective-permute-start(bf16[4,1,16,128]{3,2,1,0:T(8,128)(2,1)S(1)} %get-tuple-element.35), channel_id=1, source_target_pairs={{1,0},{2,1},{3,2},{5,4},{6,5},{7,6},{9,8},{10,9},{11,10},{13,12},{... | collective-permute-start | bytes 49160 | tf_op jit(solution)/shard_map/ppermute | solution.py:20
  28.6 6.3 %collective-permute-start.7 = (bf16[4,1,16,128]{3,2,1,0:T(8,128)(2,1)S(1)}, bf16[4,1,16,128]{3,2,1,0:T(8,128)(2,1)S(1)}, u32[]{:S(2)}, u32[]{:S(2)}) collective-permute-start(bf16[4,1,16,128]{3,2,1,0:T(8,128)(2,1)S(1)} %get-tuple-element.36), channel_id=1, source_target_pairs={{0,1},{1,2},{2,3},{4,5},{5,6},{6,7},{8,9},{9,10},{10,11},{12,13},{... | collective-permute-start | bytes 49160 | tf_op jit(solution)/shard_map/ppermute | solution.py:19
  36.7 5.0 %collective-permute-start.8 = (bf16[1,8,16,128]{3,2,1,0:T(8,128)(2,1)S(1)}, bf16[1,8,16,128]{3,2,1,0:T(8,128)(2,1)S(1)}, u32[]{:S(2)}, u32[]{:S(2)}) collective-permute-start(bf16[1,8,16,128]{3,2,1,0:T(8,128)(2,1)S(1)} %get-tuple-element.41), channel_id=1, source_target_pairs={{0,4},{4,8},{8,12},{12,16},{16,20},{20,24},{24,28},{28,32},{32,36}... | collective-permute-start | bytes 98312 | tf_op jit(solution)/shard_map/ppermute | solution.py:19
  40.3 3.5 %collective-permute-start.9 = (bf16[1,8,16,128]{3,2,1,0:T(8,128)(2,1)S(1)}, bf16[1,8,16,128]{3,2,1,0:T(8,128)(2,1)S(1)}, u32[]{:S(2)}, u32[]{:S(2)}) collective-permute-start(bf16[1,8,16,128]{3,2,1,0:T(8,128)(2,1)S(1)} %get-tuple-element.42), channel_id=1, source_target_pairs={{4,0},{8,4},{12,8},{16,12},{20,16},{24,20},{28,24},{32,28},{36,32}... | collective-permute-start | bytes 98312 | tf_op jit(solution)/shard_map/ppermute | solution.py:20
  43.8 6.1 %collective-permute-start.10 = (bf16[4,1,16,128]{3,2,1,0:T(8,128)(2,1)S(1)}, bf16[4,1,16,128]{3,2,1,0:T(8,128)(2,1)S(1)}, u32[]{:S(2)}, u32[]{:S(2)}) collective-permute-start(bf16[4,1,16,128]{3,2,1,0:T(8,128)(2,1)S(1)} %get-tuple-element.31), channel_id=1, source_target_pairs={{1,0},{2,1},{3,2},{5,4},{6,5},{7,6},{9,8},{10,9},{11,10},{13,12},{... | collective-permute-start | bytes 49160 | tf_op jit(solution)/shard_map/ppermute | solution.py:20
  45.1 6.3 %collective-permute-start.11 = (bf16[4,1,16,128]{3,2,1,0:T(8,128)(2,1)S(1)}, bf16[4,1,16,128]{3,2,1,0:T(8,128)(2,1)S(1)}, u32[]{:S(2)}, u32[]{:S(2)}) collective-permute-start(bf16[4,1,16,128]{3,2,1,0:T(8,128)(2,1)S(1)} %get-tuple-element.32), channel_id=1, source_target_pairs={{0,1},{1,2},{2,3},{4,5},{5,6},{6,7},{8,9},{9,10},{10,11},{12,13},{... | collective-permute-start | bytes 49160 | tf_op jit(solution)/shard_map/ppermute | solution.py:19
  52.1 14.3 %copy-start.2 = (f32[6,5]{1,0:T(8,128)S(1)}, f32[6,5]{1,0:T(8,128)}, u32[]{:S(2)}) copy-start(f32[6,5]{1,0:T(8,128)} %param.14) | copy-start | bytes 364
  53.1 5.0 %collective-permute-start.12 = (bf16[1,8,16,128]{3,2,1,0:T(8,128)(2,1)S(1)}, bf16[1,8,16,128]{3,2,1,0:T(8,128)(2,1)S(1)}, u32[]{:S(2)}, u32[]{:S(2)}) collective-permute-start(bf16[1,8,16,128]{3,2,1,0:T(8,128)(2,1)S(1)} %get-tuple-element.39), channel_id=1, source_target_pairs={{0,4},{4,8},{8,12},{12,16},{16,20},{20,24},{24,28},{28,32},{32,36}... | collective-permute-start | bytes 98312 | tf_op jit(solution)/shard_map/ppermute | solution.py:19
  56.8 3.5 %collective-permute-start.13 = (bf16[1,8,16,128]{3,2,1,0:T(8,128)(2,1)S(1)}, bf16[1,8,16,128]{3,2,1,0:T(8,128)(2,1)S(1)}, u32[]{:S(2)}, u32[]{:S(2)}) collective-permute-start(bf16[1,8,16,128]{3,2,1,0:T(8,128)(2,1)S(1)} %get-tuple-element.40), channel_id=1, source_target_pairs={{4,0},{8,4},{12,8},{16,12},{20,16},{24,20},{28,24},{32,28},{36,32}... | collective-permute-start | bytes 98312 | tf_op jit(solution)/shard_map/ppermute | solution.py:20
  60.3 6.4 %collective-permute-start.14 = (bf16[4,1,16,128]{3,2,1,0:T(8,128)(2,1)S(1)}, bf16[4,1,16,128]{3,2,1,0:T(8,128)(2,1)S(1)}, u32[]{:S(2)}, u32[]{:S(2)}) collective-permute-start(bf16[4,1,16,128]{3,2,1,0:T(8,128)(2,1)S(1)} %get-tuple-element.27), channel_id=1, source_target_pairs={{1,0},{2,1},{3,2},{5,4},{6,5},{7,6},{9,8},{10,9},{11,10},{13,12},{... | collective-permute-start | bytes 49160 | tf_op jit(solution)/shard_map/ppermute | solution.py:20
  61.6 6.3 %collective-permute-start.15 = (bf16[4,1,16,128]{3,2,1,0:T(8,128)(2,1)S(1)}, bf16[4,1,16,128]{3,2,1,0:T(8,128)(2,1)S(1)}, u32[]{:S(2)}, u32[]{:S(2)}) collective-permute-start(bf16[4,1,16,128]{3,2,1,0:T(8,128)(2,1)S(1)} %get-tuple-element.28), channel_id=1, source_target_pairs={{0,1},{1,2},{2,3},{4,5},{5,6},{6,7},{8,9},{9,10},{10,11},{12,13},{... | collective-permute-start | bytes 49160 | tf_op jit(solution)/shard_map/ppermute | solution.py:19
